TPU v7x, 32 devices: a whole 2x2x4 slice. The times are simulated.
32 devices in a mesh: seq: 8 (over y, x, core), dp: 4 (over z).
Axes of the slice: x: 2, y: 2, z: 4, core: 2. Of those that a mesh axis runs over, the one named last changes fastest.
Arguments:
- layer_input: bfloat16 [4, 2048, 2560], P('dp', 'seq'), may hold values from -14400 to 14400
- scan_input: bfloat16 [4, 2048, 2560], P('dp', 'seq'), may hold values from -0.75 to 0.75
- scan_cotangent: bfloat16 [4, 2048, 2560], P('dp', 'seq'), may hold values from -0.0625 to 0.0625
- step_size: float32 [4, 40, 2048], P('dp', None, 'seq'), may hold values from 0.5 to 2
- log_decay: float32 [4, 40, 2048], P('dp', None, 'seq'), may hold values from -2.25 to 0
- state_inputs: bfloat16 [4, 2048, 256], P('dp', 'seq'), may hold values from -4 to 4
- entry_state: bfloat16 [4, 8, 2560, 128], P('dp', 'seq'), may hold values from -8 to 8
Outputs:
- state_input_grad: bfloat16 [4, 2048, 256], P('dp', 'seq')
- weight_grad: float32 [2560, 256], P(('seq', 'dp'))
All inputs are finite; a program needn't handle non-finite values. Where the computation divides by a largest or mean magnitude, that divisor is 1e-20 or more.
Results may differ from a plain program's by a relative error of at most 0.013.
Values may be sent and summed in bfloat16 or wider, within the bound.
A program may use at most 128 MiB of HBM per device.

v0:
```python
import jax
import jax.numpy as jnp
from jax import lax
from jax.sharding import PartitionSpec as P

STRETCH = 256


epsilon = 1e-06


def entering(x, axis, combine, identity):
    length, place = (lax.axis_size(axis), lax.axis_index(axis))
    everything = jax.tree.map(lambda part: lax.all_gather(part, axis), x)
    start = jax.tree.map(
        lambda part, zero: jnp.broadcast_to(jnp.asarray(zero, part.dtype), part.shape), x, identity
    )

    def hop(k, before):
        at = length - 1 - k
        reached = at > place
        new = combine(before, jax.tree.map(lambda part: part[at], everything))
        return jax.tree.map(lambda a, b: jnp.where(reached, a, b), new, before)

    return lax.fori_loop(0, length, hop, start)


def silu_slope(value):
    sigma = jax.nn.sigmoid(value)
    return sigma * (1.0 + value * (1.0 - sigma))


def compose(earlier, later):
    return (earlier[0] * later[0], later[1] + later[0][:, :, None, None] * earlier[1])


def block_summary(pieces):
    inputs, cotangents, steps, cumulative, writes, reads = pieces
    weighted_cot = (cotangents * jnp.exp(cumulative).T[:, :, None]).astype(jnp.bfloat16)
    weighted_in = (
        inputs * (steps * jnp.exp(cumulative[:, -1:] - cumulative)).T[:, :, None]
    ).astype(jnp.bfloat16)
    from_later = jnp.einsum("thp,tn->hpn", weighted_cot, reads, preferred_element_type=jnp.float32)
    from_earlier = jnp.einsum(
        "thp,tn->hpn", weighted_in, writes, preferred_element_type=jnp.float32
    )
    return (weighted_cot, weighted_in, from_later, from_earlier, jnp.exp(cumulative[:, -1]))


def block_inner(pieces):
    inputs, cotangents, steps, cumulative, writes, reads = pieces
    length = inputs.shape[0]
    later = lax.broadcasted_iota(jnp.int32, (length, length), 0) >= lax.broadcasted_iota(
        jnp.int32, (length, length), 1
    )
    scores = jnp.einsum("shp,thp->hst", cotangents, inputs, preferred_element_type=jnp.float32)
    spread = jnp.where(later[None], cumulative[:, :, None] - cumulative[:, None, :], 0.0)
    decay = jnp.where(later[None], jnp.exp(spread), 0.0)
    mixing = (scores * decay * steps[:, None, :]).astype(jnp.bfloat16)
    inner_write = jnp.einsum("hst,sn->tn", mixing, reads, preferred_element_type=jnp.float32)
    inner_read = jnp.einsum("hst,tn->sn", mixing, writes, preferred_element_type=jnp.float32)
    return (inner_write, inner_read)


def block_both(pieces):
    return block_summary(pieces) + block_inner(pieces)


def on_device(
    layer_input, scan_input, scan_cotangent, step_size, log_decay, state_inputs, entry_state
):
    seq_local, tokens, width = layer_input.shape
    heads = step_size.shape[1]
    channels = scan_input.shape[2]
    head_size = channels // heads
    states = state_inputs.shape[2] // 2
    blocks = tokens // STRETCH
    count = seq_local * blocks
    local_peaks = jnp.max(jnp.abs(layer_input), axis=(0, 1))
    peaks = lax.pmax(local_peaks, ("seq", "dp")).astype(jnp.float32)
    inputs = scan_input.reshape(count, STRETCH, heads, head_size)
    cotangents = scan_cotangent.reshape(count, STRETCH, heads, head_size)
    steps = (
        step_size.reshape(seq_local, heads, blocks, STRETCH)
        .transpose(0, 2, 1, 3)
        .reshape(count, heads, STRETCH)
    )
    decays = (
        log_decay.reshape(seq_local, heads, blocks, STRETCH)
        .transpose(0, 2, 1, 3)
        .reshape(count, heads, STRETCH)
    )
    cumulative = jnp.cumsum(decays, axis=2)
    preact = state_inputs.astype(jnp.float32)
    activated = jax.nn.silu(preact).astype(jnp.bfloat16)
    writes = activated[:, :, :states]
    reads = activated[:, :, states:]
    pieces = (inputs, cotangents, steps, cumulative, writes, reads)
    weighted_cot, weighted_in, from_later, from_earlier, totals, inner_write, inner_read = lax.map(
        block_both, pieces
    )
    from_later = from_later.reshape(seq_local, blocks, heads, head_size, states)
    from_earlier = from_earlier.reshape(seq_local, blocks, heads, head_size, states)
    totals = totals.reshape(seq_local, blocks, heads)
    later_sum = from_later[:, blocks - 1]
    device_decay = jnp.prod(totals, axis=1)
    identity = (jnp.ones_like(device_decay), jnp.zeros_like(later_sum))
    beyond = entering((device_decay, later_sum), "seq", compose, identity)[1]
    weighted_in = weighted_in.reshape(seq_local, blocks, STRETCH, channels)
    weighted_cot = weighted_cot.reshape(seq_local, blocks, STRETCH, channels)
    carried_write = []
    state_now = beyond
    block_index = 0
    operand = state_now.astype(jnp.bfloat16).reshape(seq_local, channels, states)
    carried_write.append(
        jnp.einsum(
            "btk,bkn->btn", weighted_in[:, block_index], operand, preferred_element_type=jnp.float32
        )
    )
    carried_write = jnp.stack(carried_write[::-1], axis=1).reshape(seq_local, tokens, states)
    carried_read = []
    state_now = entry_state.reshape(seq_local, heads, head_size, states).astype(jnp.float32)
    block_index = 0
    operand = state_now.astype(jnp.bfloat16).reshape(seq_local, channels, states)
    carried_read.append(
        jnp.einsum(
            "btk,bkn->btn",
            weighted_cot[:, block_index],
            operand,
            preferred_element_type=jnp.float32,
        )
    )
    carried_read = jnp.stack(carried_read, axis=1).reshape(seq_local, tokens, states)
    grad_write = inner_write + carried_write
    grad_read = inner_read + carried_read
    state_input_grad = (
        jnp.concatenate([grad_write, grad_read], axis=2) * silu_slope(preact)
    ).astype(jnp.bfloat16)
    factor = 1.0 / (peaks + epsilon)
    quantized = (layer_input.reshape(seq_local * tokens, width) * factor).astype(jnp.bfloat16)
    grads = state_input_grad.reshape(seq_local * tokens, 2 * states)
    partial_rows = lax.psum_scatter(
        lax.dot_general(
            quantized, grads, (((0,), (0,)), ((), ())), preferred_element_type=jnp.float32
        ),
        "seq",
        scatter_dimension=0,
        tiled=True,
    )
    summed = lax.psum_scatter(partial_rows, "dp", scatter_dimension=0, tiled=True)
    return (state_input_grad, summed)


def solution(mesh):
    placed = (
        P("dp", "seq", None),
        P("dp", "seq", None),
        P("dp", "seq", None),
        P("dp", None, "seq"),
        P("dp", None, "seq"),
        P("dp", "seq", None),
        P("dp", "seq", None, None),
    )
    return jax.shard_map(
        on_device,
        mesh=mesh,
        in_specs=placed,
        out_specs=(P("dp", "seq", None), P(("seq", "dp"), None)),
        check_vma=False,
    )
```

profile of v0, /device:TPU:0, one launch (start us, length us, event | category | flops | bytes accessed | tf_op | source)
XLA Modules:
  0.0 184.1 jit_solution(1644296316415765843)
XLA Ops:
  7.2 0.8 copy_bitcast_fusion
  8.1 0.6 reduce-window.6
  8.6 0.2 slice_reduce_fusion
  9.0 1.0 copy.36
  10.1 1.6 copy.31
  11.8 0.8 exponential_bitcast_fusion
  12.6 0.3 fusion.1
  12.9 1.6 fusion.34
  14.6 0.6 copy-done.6
  15.2 0.6 dynamic-slice
  16.4 0.9 slice_reduce_fusion.1
  17.3 0.2 dynamic-update-slice
  17.6 15.6 %all-reduce = f32[320]{0:T(512)S(1)} all-reduce(f32[320]{0:T(512)S(1)} %dynamic-update-slice), channel_id=3, replica_groups=mesh['seq'=8,'dp'=4] {'seq'}, use_global_device_ids=true, to_apply=%add | all-reduce | flops 320 | bytes 2560
  33.2 0.7 reshape.144
  33.9 2.4 %copy.32 = bf16[1,256,2560]{1,2,0:T(8,128)(2,1)} copy(bf16[1,256,2560]{2,1,0:T(8,128)(2,1)} %param.10) | data formatting | bytes 2621440 | tf_op args[1]
  36.3 0.9 multiply_bitcast_fusion
  37.2 2.8 %fusion.2 = bf16[1,256,2560]{1,2,0:T(8,128)(2,1)} fusion(bf16[1,256,2560]{1,2,0:T(8,128)(2,1)} %copy.32, f32[256,40]{0,1:T(8,128)S(1)} %multiply_bitcast_fusion), kind=kLoop, calls=%fused_computation.8 | loop fusion | flops 1966080 | bytes 2662400 | tf_op jit(solution)/shard_map/while/body/eval_jaxpr/convert_element_type | solution.py:42
  40.0 0.2 abs_reduce_fusion
  40.1 40.4 %pmax.7 = bf16[2560]{0:T(1024)(128)(2,1)S(1)} all-reduce(bf16[2560]{0:T(1024)(128)(2,1)S(1)} %abs_reduce_fusion), channel_id=1, replica_groups=mesh['seq'=8,'dp'=4] {'seq','dp'}, use_global_device_ids=true, to_apply=%region_6.7 | all-reduce | flops 2560 | bytes 10240 | tf_op jit(solution)/shard_map/pmax | solution.py:80
  80.5 5.7 %convert_reduce_fusion = bf16[256,256]{1,0:T(8,128)(2,1)S(1)} fusion(f32[40,256]{1,0:T(8,128)} %bitcast.99, f32[40,256]{1,0:T(8,128)} %get-tuple-element.226, pred[256,256]{1,0:T(8,128)(4,1)S(1)} %iota_compare_fusion, bf16[256,40,64]{0,2,1:T(8,128)(2,1)} %bitcast.93, bf16[256,40,64]{0,2,1:T(8,128)(2,1)} %bitcast.94), kind=kOutput, calls=%fused_computation.3 | convolution fusion | flops 356450304 | bytes 2899968 | tf_op jit(solution)/shard_map/while/body/eval_jaxpr/shp,thp->hst/dot_general | solution.py:56
  86.3 0.2 fusion.33
  86.5 1.1 fusion.20
  87.5 0.2 fusion.36
  87.7 18.2 %while.11 = (s32[]{:T(128)}, f32[1,40,64,128]{3,2,1,0:T(8,128)S(1)}, s32[]{:T(128)}, f32[8,1,40,64,128]{4,3,2,1,0:T(8,128)}, f32[8,1,40]{2,1,0:T(1,128)}, /*index=5*/s32[]{:T(128)}, s32[]{:T(128)}, s32[]{:T(128)}, s32[]{:T(128)}) while((s32[]{:T(128)}, f32[1,40,64,128]{3,2,1,0:T(8,128)S(1)}, s32[]{:T(128)}, ...), condition=%wide.region_4.5_spmd.clone, body=%wide.region_3.4_spmd.clone.sunk | while | flops 1310728 | bytes 3932815 | solution.py:25
  87.8 0.6 dynamic-slice_bitcast_fusion.2
  88.4 1.6 fusion.48
  90.0 0.6 dynamic-slice_bitcast_fusion.2
  90.7 1.6 fusion.48
  92.3 0.7 dynamic-slice_bitcast_fusion.2
  93.0 1.6 fusion.48
  94.6 0.7 dynamic-slice_bitcast_fusion.2
  95.3 1.6 fusion.48
  97.0 0.6 dynamic-slice_bitcast_fusion.2
  97.6 1.6 fusion.48
  99.2 0.6 dynamic-slice_bitcast_fusion.2
  99.8 1.6 fusion.48
  101.5 0.6 dynamic-slice_bitcast_fusion.2
  102.1 1.6 fusion.48
  103.7 0.6 dynamic-slice_bitcast_fusion.2
  104.4 1.6 fusion.48
  106.1 1.2 copy-done.3
  107.3 0.4 fusion.14
  107.7 0.1 fusion.31
  107.8 0.8 copy-done.2
  108.6 2.1 %fusion.4 = f32[2560,256]{1,0:T(8,128)} fusion(bf16[1,256,2560]{2,1,0:T(8,128)(2,1)S(1)} %copy-done.2, f32[2560]{0:T(1024)S(1)} %add_divide_fusion, bf16[1,256,256]{1,2,0:T(8,128)(2,1)S(1)} %fusion.31), kind=kOutput, calls=%fused_computation.11 | convolution fusion | flops 337510400 | bytes 4073472 | tf_op jit(solution)/shard_map/dot_general | solution.py:143
  110.8 43.4 %reduce-scatter.3.cloned.1.call-done = f32[320,256]{1,0:T(8,128)} async-done(((f32[2560,256]{1,0:T(8,128)}), f32[320,256]{1,0:T(8,128)}) %reduce-scatter.3.cloned.1.call-update) | async-done | bytes 327696 | tf_op jit(solution)/shard_map/reduce_scatter | solution.py:142
  154.2 0.8 copy.41
  155.0 22.6 %reduce-scatter.5.cloned.1.call-done = f32[80,256]{1,0:T(8,128)} async-done(((f32[320,256]{1,0:T(8,128)}), f32[80,256]{1,0:T(8,128)}) %reduce-scatter.5.cloned.1.call-update) | async-done | bytes 81936 | tf_op jit(solution)/shard_map/reduce_scatter | solution.py:150
  (29 shorter events, 0.7 us)
Async XLA Ops:
  7.2 79.3 %copy-start = (bf16[1,1,2560,128]{3,2,1,0:T(8,128)(2,1)S(1)}, bf16[1,1,2560,128]{3,2,1,0:T(8,128)(2,1)}, u32[]{:S(2)}) copy-start(bf16[1,1,2560,128]{3,2,1,0:T(8,128)(2,1)} %param.15) | copy-start | bytes 1966084
  7.2 80.5 %all-gather.4.cloned.1.call-start = ((), (), s32[]{:S(2)}) async-start(), calls=%async_computation.4 | async-start | bytes 11796480 | tf_op jit(solution)/shard_map/all_gather | solution.py:14
  11.7 1.2 copy-start.4
  14.5 0.7 copy-start.6
  14.5 139.7 %reduce-scatter.3.cloned.1.call-start = ((), (), s32[]{:S(2)}) async-start(), calls=%async_computation.2 | async-start | bytes 2949120 | tf_op jit(solution)/shard_map/reduce_scatter | solution.py:142
  37.2 2.8 %copy-start.1 = (bf16[1,256,2560]{2,1,0:T(8,128)(2,1)S(1)}, bf16[1,256,2560]{2,1,0:T(8,128)(2,1)}, u32[]{:S(2)}) copy-start(bf16[1,256,2560]{2,1,0:T(8,128)(2,1)} %param.9) | copy-start | bytes 3932164
  106.0 1.3 copy-start.3
  106.1 1.6 copy-start.5
  107.3 1.3 copy-start.2
  110.7 66.9 %reduce-scatter.5.cloned.1.call-start = ((), (), s32[]{:S(2)}) async-start(), calls=%async_computation.3 | async-start | bytes 409600 | tf_op jit(solution)/shard_map/reduce_scatter | solution.py:150
Sparse Core Ops, SparseCore 0:
  14.7 66.5 all-gather.3
  110.9 43.3 reduce-scatter.2
  157.1 20.4 reduce-scatter.4
where the time goes:
time: 185 us; the launch traced here: 184 us
  waiting for transfers between devices  66.1 us (36%)
  blocking collectives  56 us (30%)
  other arithmetic  18.8 us (10%)
  local copies, waits for them, and re-layouts  17.1 us (9%)
  between operations  14.6 us (8%)
  matrix products  11.3 us (6%)
    reduce_scatter x1, waiting for transfers between devices, on_device(): lax.psum_scatter(lax.dot_general(quantized, grads, (((0,), (0,)), ((), ()...  43.4 us
    pmax x1, blocking collectives, on_device(): peaks = lax.pmax(local_peaks, ('seq', 'dp')).astype(jnp.float32)  40.4 us
    reduce_scatter x1, waiting for transfers between devices, on_device(): lax.psum_scatter(partial_rows, 'dp', scatter_dimension=0, tiled=True)  22.6 us
    unnamed x1, blocking collectives  15.6 us
    select_n x8, other arithmetic, hop(): return jax.tree.map(lambda a, b: jnp.where(reached, a, b), new, before)  12.9 us
    unnamed x21, local copies, waits for them, and re-layouts  9.15 us
    dot_general x1, matrix products, block_inner(): jnp.einsum('shp,thp->hst', cotangents, inputs, preferred_element_type=jnp...  5.73 us
    mul x8, local copies, waits for them, and re-layouts, compose(): later[0][:, :, None, None] * earlier[1]  5.08 us
  transfers between devices with their start and end apart: 3, of which 2 were waited for; matrix products, arithmetic and copies ran while one was open for 9% of the time, Pallas kernels for 0%

commit v1 on v0

v1 whole, which is shorter than its diff:
```python
import functools
import math

import jax
import jax.numpy as jnp
from jax import lax
from jax.experimental import pallas as pl
from jax.experimental.pallas import tpu as pltpu
from jax.sharding import PartitionSpec as P

MESH = pl.DeviceIdType.MESH
F32 = jnp.float32
BF16 = jnp.bfloat16
LANES = 128
LOG2E = 1.4426950408889634
EPSILON = 1e-06


def nt(a, b, precision=None):
    return lax.dot_general(
        a, b, (((1,), (1,)), ((), ())), preferred_element_type=F32, precision=precision
    )


def tn(a, b):
    return lax.dot_general(a, b, (((0,), (0,)), ((), ())), preferred_element_type=F32)


def nn(a, b):
    return jnp.dot(a, b, preferred_element_type=F32)


class Sizes:
    def __init__(self, n_seq, n_dp, tokens, width, channels, heads, states):
        self.n_seq, self.n_dp, self.tokens, self.width = n_seq, n_dp, tokens, width
        self.channels, self.heads, self.states = channels, heads, states
        self.head = channels // heads
        self.bits = n_seq.bit_length() - 1
        self.half_heads = heads // 2
        self.half_pairs = channels // LANES // 2
        self.per = LANES // self.head
        self.chunks = max(c for c in range(1, 6) if self.half_pairs % c == 0)
        self.chunk_pairs = self.half_pairs // self.chunks
        self.chunk_rows = self.chunk_pairs * LANES
        self.chunk_heads = self.chunk_rows // self.head
        self.wide = width // LANES
        self.wide_pad = -(-self.wide // 16) * 16
        self.rows_seq = width // n_seq
        self.rows = self.rows_seq // n_dp


def kernel(
    z,
    layer_hbm, scan_hbm, cot_hbm, entry_hbm, step_ref, decay_ref, state_ref,
    grad_out, weight_out,
    layer, scan, cot, entry, local_sem,
    crow, ccol, wcol, wcot, win,
    fsend, frecv, fown, fhigh, fsum, bsum, dsend, drecv, beyond, bsend, brecv,
    fsem_s, fsem_r, dsem_s, dsem_r, bsem_s, bsem_r,
    mix, part, wsend, wrecv, wsem_s, wsem_r, zsend, zrecv, zown, zsem_s, zsem_r,
    peak, peak_send, peak_recv, peak_send2, peak_recv2, pkcol,
    psem_s, psem_r, qsem_s, qsem_r,
):
    n, m, t = z.n_seq, z.n_dp, z.tokens
    me, dz = lax.axis_index("seq"), lax.axis_index("dp")
    bit = [lax.rem(me // (1 << b), 2) for b in range(z.bits)]
    mate = [me + (1 - 2 * bit[b]) * (1 << b) for b in range(z.bits)]
    mine, other = bit[0], 1 - bit[0]

    locals_ = [
        pltpu.make_async_copy(src, dst, local_sem.at[i])
        for i, (src, dst) in enumerate(
            ((cot_hbm, cot), (scan_hbm, scan), (layer_hbm, layer), (entry_hbm, entry))
        )
    ]
    for c in locals_:
        c.start()

    barrier = pltpu.get_barrier_semaphore()
    for o in range(1, n):
        pl.semaphore_signal(
            barrier, inc=1, device_id={"seq": lax.rem(me + o, n), "dp": dz}, device_id_type=MESH
        )
    for o in range(1, m):
        pl.semaphore_signal(
            barrier, inc=1, device_id={"seq": me, "dp": lax.rem(dz + o, m)}, device_id_type=MESH
        )

    decay = decay_ref[...] * LOG2E
    row = lax.broadcasted_iota(jnp.int32, (t, t), 0)
    col = lax.broadcasted_iota(jnp.int32, (t, t), 1)
    lower = jnp.where(col <= row, 1.0, 0.0).astype(F32)
    high = lax.Precision.HIGHEST
    cum = nt(decay, lower, high)
    cum_t = nt(lower, decay, high)
    steps = step_ref[...]
    crow[...] = cum - jnp.log2(steps)
    weight_t = jnp.transpose(steps) * jnp.exp2(cum_t[t - 1 : t, :] - cum_t)
    lane = lax.broadcasted_iota(jnp.int32, (t, LANES), 1)
    total = jnp.broadcast_to(jnp.exp2(cum[:, t - 1 : t]), (z.heads, LANES))
    tot = [total[: z.half_heads], total[z.half_heads :]]
    tot_mine = jnp.where(mine == 1, tot[1], tot[0])
    dsend[0] = jnp.where(mine == 1, tot[0], tot[1])
    for h in range(z.heads):
        ccol[h] = jnp.broadcast_to(cum_t[:, h : h + 1], (t, LANES))

    pre = state_ref[...].astype(F32)
    sigma = 1.0 / (1.0 + jnp.exp(-pre))
    activated = (pre * sigma).astype(BF16)
    writes, reads = activated[:, : z.states], activated[:, z.states :]

    def by_head(g, table):
        value = table[g * z.per]
        for k in range(1, z.per):
            value = jnp.where(lane >= k * z.head, table[g * z.per + k], value)
        return value

    def later(g):
        at = pl.ds(pl.multiple_of(g * LANES, LANES), LANES)
        weighted = (cot[:, at].astype(F32) * jnp.exp2(by_head(g, ccol))).astype(BF16)
        wcot[:, at] = weighted
        return tn(weighted, reads)

    def remote(src, dst, s_sem, r_sem, seq, dp):
        return pltpu.make_async_remote_copy(
            src_ref=src, dst_ref=dst, send_sem=s_sem, recv_sem=r_sem,
            device_id={"seq": seq, "dp": dp}, device_id_type=MESH,
        )

    def f_copy(b, c):
        return remote(
            fsend.at[b, c], frecv.at[b, c], fsem_s.at[b, c], fsem_r.at[b, c], mate[b], dz
        )

    def d_copy(b):
        return remote(dsend.at[b], drecv.at[b], dsem_s.at[b], dsem_r.at[b], mate[b], dz)

    def spread(d, c):
        return jnp.concatenate(
            [
                jnp.broadcast_to(d[h : h + 1, :], (z.head, LANES))
                for h in range(c * z.chunk_heads, (c + 1) * z.chunk_heads)
            ],
            axis=0,
        )

    started = []

    def go(copy):
        copy.start()
        started.append(copy)
        return copy

    locals_[0].wait()
    for c in range(z.chunks):
        for p in range(z.chunk_pairs):
            g = other * z.half_pairs + c * z.chunk_pairs + p
            fsend[0, c, p * LANES : (p + 1) * LANES, :] = later(g).astype(BF16)
        if c == 0:
            pl.semaphore_wait(barrier, n - 1 + m - 1)
            go(d_copy(0))
        go(f_copy(0, c))
    for c in range(z.chunks):
        for p in range(z.chunk_pairs):
            g = mine * z.half_pairs + c * z.chunk_pairs + p
            fown[c, p * LANES : (p + 1) * LANES, :] = later(g)

    d_copy(0).wait_recv()
    tot_other = drecv[0]
    tot_low = jnp.where(mine == 1, tot_other, tot_mine)
    tot_high = jnp.where(mine == 1, tot_mine, tot_other)
    d_now = tot_low * tot_high
    if z.bits > 1:
        dsend[1] = d_now
        go(d_copy(1))
    for c in range(z.chunks):
        f_copy(0, c).wait_recv()
        own, far = fown[c], frecv[0, c].astype(F32)
        up = jnp.where(mine == 1, own, far)
        fhigh[c] = up
        value = jnp.where(mine == 1, far, own) + spread(tot_low, c) * up
        bsum[c] = jnp.zeros_like(value)
        fsum[c] = value
        if z.bits > 1:
            fsend[1, c] = value.astype(BF16)
            go(f_copy(1, c))

    locals_[2].wait()
    peak[...] = jnp.zeros_like(peak)
    for j in range(z.wide):
        block = layer[:, j * LANES : (j + 1) * LANES].astype(F32)
        peak[j : j + 1, :] = jnp.max(jnp.abs(block), axis=0, keepdims=True)
    peak_send[...] = peak[...].astype(BF16)
    peak_copies = [
        go(remote(peak_send, peak_recv.at[o - 1], psem_s.at[o - 1], psem_r.at[o - 1],
                  lax.rem(me + o, n), dz))
        for o in range(1, n)
    ]

    locals_[1].wait()
    for h in range(z.heads):
        wcol[h] = jnp.broadcast_to(weight_t[:, h : h + 1], (t, LANES))
    mix[...] = jnp.zeros_like(mix)
    hf = t // 2
    keep = row[:hf, :hf] >= col[:hf, :hf]

    def mixing(g, carry):
        at = pl.ds(pl.multiple_of(g * LANES, LANES), LANES)
        c_pair, s_pair = cot[:, at], scan[:, at]
        win[:, at] = (s_pair.astype(F32) * by_head(g, wcol)).astype(BF16)
        for k in range(z.per):
            h = g * z.per + k
            inside = (lane >= k * z.head) & (lane < (k + 1) * z.head)
            c_head = jnp.where(inside, c_pair.astype(F32), 0.0).astype(BF16)
            rows = crow[pl.ds(h, 1), :]
            for s in range(2):
                scores = nt(c_head[s * hf : (s + 1) * hf], s_pair[: (s + 1) * hf])
                for r in range(s + 1):
                    cols = ccol[h, s * hf : (s + 1) * hf, :]
                    cut = slice(r * hf, (r + 1) * hf)
                    spread_ = cols - rows[:, cut]
                    if s == r:
                        spread_ = jnp.where(keep, spread_, -1e30)
                    mix[s * hf : (s + 1) * hf, cut] += scores[:, cut] * jnp.exp2(spread_)
        return carry

    lax.fori_loop(0, z.heads // z.per, mixing, 0)

    e_now = None
    for b in range(1, z.bits):
        d_copy(b).wait_recv()
        d_far = drecv[b]
        d_low = jnp.where(bit[b] == 1, d_far, d_now)
        last = b == z.bits - 1
        if not last:
            dsend[b + 1] = d_now * d_far
            go(d_copy(b + 1))
        for c in range(z.chunks):
            f_copy(b, c).wait_recv()
            far = frecv[b, c].astype(F32)
            scaled = far if e_now is None else spread(e_now, c) * far
            gained = bsum[c] + jnp.where(bit[b] == 1, jnp.zeros_like(scaled), scaled)
            if not last:
                bsum[c] = gained
                own = fsum[c]
                value = jnp.where(bit[b] == 1, far, own) + spread(d_low, c) * jnp.where(
                    bit[b] == 1, own, far
                )
                fsum[c] = value
                fsend[b + 1, c] = value.astype(BF16)
                go(f_copy(b + 1, c))
            else:
                bsum[c] = gained
        one = jnp.ones_like(d_far) if e_now is None else e_now
        e_now = jnp.where(bit[b] == 1, one, one * d_far)
        d_now = d_now * d_far
    for o in range(1, n):
        peak_copies[o - 1].wait_recv()

    b_copies = []
    mixed = mix[...].astype(BF16)
    grad_write = tn(mixed, reads)
    for c in range(z.chunks):
        top = bsum[c]
        low = fhigh[c] + spread(tot_high, c) * top
        beyond[c] = jnp.where(mine == 1, top, low).astype(BF16)
        bsend[c] = jnp.where(mine == 1, low, top).astype(BF16)
        b_copies.append(
            go(remote(bsend.at[c], brecv.at[c], bsem_s.at[c], bsem_r.at[c], mate[0], dz))
        )

    slope = sigma * (1.0 + pre * (1.0 - sigma))
    order = {1: list(range(z.bits)), 0: [0] + list(range(1, z.bits))[::-1]}
    states = z.states

    def place(r, q):
        s = 0
        for k, b in enumerate(order[q]):
            s += ((r >> (z.bits - 1 - k)) & 1) << b
        return s

    offset = [sum(n >> (k + 1) for k in range(i)) for i in range(z.bits)]

    def w_copy(q, k):
        size = n >> (k + 1)
        at = pl.ds(offset[k], size)
        return remote(
            wsend.at[q, at], wrecv.at[q, at], wsem_s.at[q, k], wsem_r.at[q, k],
            mate[order[q][k]], dz,
        )

    def w_send(q, k, start):
        size = n >> (k + 1)
        b = bit[order[q][k]]
        away, kept = start + (1 - b) * size, start + b * size
        for j in range(size):
            wsend[q, offset[k] + j] = part[q, away + j].astype(BF16)
        go(w_copy(q, k))
        return kept

    def w_begin(q, grads):
        product = tn(layer[...], grads)
        for r in range(n):
            s = place(r, q)
            part[q, r] = product[s * z.rows_seq : (s + 1) * z.rows_seq, :]
        return w_send(q, 0, 0)

    def w_step(q, k, start):
        w_copy(q, k).wait_recv()
        size = n >> (k + 1)
        for j in range(size):
            part[q, start + j] += wrecv[q, offset[k] + j].astype(F32)
        if k + 1 < z.bits:
            return w_send(q, k + 1, start)
        scale = 1.0 / (pkcol[pl.ds(pl.multiple_of(me * z.rows_seq, 8), z.rows_seq), :] + EPSILON)
        value = part[q, start] * scale
        for d in range(m):
            piece = value[d * z.rows : (d + 1) * z.rows, :]
            zsend[q, d] = piece.astype(BF16)
            zown[q, d] = piece
        for o in range(1, m):
            go(z_copy(q, o))
        return start

    def z_copy(q, o):
        to = lax.rem(dz + o, m)
        return remote(
            zsend.at[q, to], zrecv.at[q, o - 1], zsem_s.at[q, o - 1], zsem_r.at[q, o - 1], me, to
        )

    def w_end(q):
        value = zown[q, dz]
        for o in range(1, m):
            z_copy(q, o).wait_recv()
            value += zrecv[q, o - 1].astype(F32)
        weight_out[:, q * states : (q + 1) * states] = value

    locals_[3].wait()
    grad_read = nn(mixed, writes) + nn(wcot[...], entry[...])
    reads_grad = (grad_read * slope[:, states:]).astype(BF16)
    grad_out[:, states:] = reads_grad
    at_read = w_begin(1, reads_grad)

    top = peak[...]
    for o in range(1, n):
        top = jnp.maximum(top, peak_recv[o - 1].astype(F32))
    peak_send2[...] = top.astype(BF16)
    peak_copies2 = [
        go(remote(peak_send2, peak_recv2.at[o - 1], qsem_s.at[o - 1], qsem_r.at[o - 1],
                  me, lax.rem(dz + o, m)))
        for o in range(1, m)
    ]

    def carried(half, c, state):
        width = z.chunk_rows
        at = pl.multiple_of(half * (z.channels // 2) + c * width, LANES)
        return nn(win[:, pl.ds(at, width)], state)

    for c in range(z.chunks):
        grad_write += carried(mine, c, beyond[c])
    for c in range(z.chunks):
        b_copies[c].wait_recv()
        grad_write += carried(other, c, brecv[c])
    writes_grad = (grad_write * slope[:, :states]).astype(BF16)
    grad_out[:, :states] = writes_grad
    at_write = w_begin(0, writes_grad)

    for o in range(1, m):
        peak_copies2[o - 1].wait_recv()
        top = jnp.maximum(top, peak_recv2[o - 1].astype(F32))
    unit = jnp.where(
        lax.broadcasted_iota(jnp.int32, (LANES, LANES), 0)
        == lax.broadcasted_iota(jnp.int32, (LANES, LANES), 1), 1.0, 0.0,
    ).astype(BF16)
    turned = nt(unit, top.astype(BF16))
    for j in range(z.wide):
        pkcol[j * LANES : (j + 1) * LANES, :] = jnp.broadcast_to(
            turned[:, j : j + 1], (LANES, LANES)
        )

    for k in range(z.bits):
        at_read = w_step(1, k, at_read)
        at_write = w_step(0, k, at_write)
    w_end(1)
    w_end(0)
    for copy in started:
        copy.wait_send()


def solution(mesh):
    n_seq, n_dp = mesh.shape["seq"], mesh.shape["dp"]

    def on_device(
        layer_input, scan_input, scan_cotangent, step_size, log_decay, state_inputs, entry_state
    ):
        tokens, width = layer_input.shape[1:]
        channels, heads = scan_input.shape[2], step_size.shape[1]
        states = state_inputs.shape[2] // 2
        z = Sizes(n_seq, n_dp, tokens, width, channels, heads, states)
        dma = pltpu.SemaphoreType.DMA
        chunk = (z.chunks, z.chunk_rows, states)
        steps_w = n_seq - 1
        peers, mates = max(n_dp - 1, 1), max(n_seq - 1, 1)
        peak = (z.wide_pad, LANES)
        block = (z.rows_seq, states)
        piece = (z.rows, states)
        V = pltpu.VMEM
        scratch = [
            V((tokens, width), BF16), V((tokens, channels), BF16), V((tokens, channels), BF16),
            V((channels, states), BF16), dma((4,)),
            V((heads, tokens), F32), V((heads, tokens, LANES), F32),
            V((heads, tokens, LANES), F32), V((tokens, channels), BF16),
            V((tokens, channels), BF16),
            V((z.bits,) + chunk, BF16), V((z.bits,) + chunk, BF16), V(chunk, F32), V(chunk, F32),
            V(chunk, F32), V(chunk, F32), V((z.bits, z.half_heads, LANES), F32),
            V((z.bits, z.half_heads, LANES), F32), V(chunk, BF16), V(chunk, BF16), V(chunk, BF16),
            dma((z.bits, z.chunks)), dma((z.bits, z.chunks)), dma((z.bits,)), dma((z.bits,)),
            dma((z.chunks,)), dma((z.chunks,)),
            V((tokens, tokens), F32), V((2, n_seq) + block, F32),
            V((2, steps_w) + block, BF16), V((2, steps_w) + block, BF16),
            dma((2, z.bits)), dma((2, z.bits)),
            V((2, n_dp) + piece, BF16), V((2, peers) + piece, BF16), V((2, n_dp) + piece, F32),
            dma((2, peers)), dma((2, peers)),
            V(peak, F32), V(peak, BF16), V((mates,) + peak, BF16), V(peak, BF16),
            V((peers,) + peak, BF16), V((width, LANES), F32),
            dma((mates,)), dma((mates,)), dma((peers,)), dma((peers,)),
        ]
        any_ = pl.BlockSpec(memory_space=pl.ANY)
        vmem = pl.BlockSpec(memory_space=pltpu.VMEM)
        grads, weights = pl.pallas_call(
            functools.partial(kernel, z),
            out_shape=(
                jax.ShapeDtypeStruct((tokens, 2 * states), BF16),
                jax.ShapeDtypeStruct((z.rows, 2 * states), F32),
            ),
            in_specs=[any_] * 4 + [vmem] * 3,
            out_specs=(vmem, vmem),
            scratch_shapes=scratch,
            compiler_params=pltpu.CompilerParams(
                collective_id=0, has_side_effects=True, vmem_limit_bytes=60 * 1024 * 1024
            ),
        )(
            layer_input[0], scan_input[0], scan_cotangent[0], entry_state[0, 0],
            step_size[0], log_decay[0], state_inputs[0],
        )
        return grads[None], weights

    placed = (
        P("dp", "seq", None),
        P("dp", "seq", None),
        P("dp", "seq", None),
        P("dp", None, "seq"),
        P("dp", None, "seq"),
        P("dp", "seq", None),
        P("dp", "seq", None, None),
    )
    return jax.shard_map(
        on_device,
        mesh=mesh,
        in_specs=placed,
        out_specs=(P("dp", "seq", None), P(("seq", "dp"), None)),
        check_vma=False,
    )
```

time: 185 us -> 49.6 us (0.27)
  waiting for transfers between devices: 66.1 us -> 0 us
  blocking collectives: 56 us -> 0 us
  Pallas kernels: 0 us -> 45.6 us
  other arithmetic: 18.8 us -> 0 us
  local copies, waits for them, and re-layouts: 17.1 us -> 3.09 us
  between operations: 14.6 us -> 0.64 us
  matrix products: 11.3 us -> 0 us
    reduce_scatter x2 -> x0, waiting for transfers between devices: 66 us -> none  [the longest x1 43.4 us: on_device(): lax.psum_scatter(lax.dot_general(quantized, grads, (((0,), (0,)), ((), ()...]
    pallas_call x0 -> x1, Pallas kernels: none -> 45.6 us  [on_device(): pl.pallas_call(functools.partial(kernel, z), out_shape=(jax.ShapeDtypeStr...]
    pmax x1 -> x0, blocking collectives: 40.4 us -> none  [on_device(): peaks = lax.pmax(local_peaks, ('seq', 'dp')).astype(jnp.float32)]
    unnamed x1 -> x0, blocking collectives: 15.6 us -> none
    select_n x8 -> x0, other arithmetic: 12.9 us -> none  [hop(): return jax.tree.map(lambda a, b: jnp.where(reached, a, b), new, before)]
    dot_general x7 -> x0, matrix products: 11.3 us -> none  [the longest x1 5.73 us: block_inner(): jnp.einsum('shp,thp->hst', cotangents, inputs, preferred_element_type=jnp...]
    unnamed x21 -> x2, local copies, waits for them, and re-layouts: 9.15 us -> 3.09 us
    mul x8 -> x0, local copies, waits for them, and re-layouts: 5.08 us -> none  [compose(): later[0][:, :, None, None] * earlier[1]]
  transfers between devices with their start and end apart: 3 -> 0, of which waited for: 2 -> 0; matrix products, arithmetic and copies ran while one was open for 9% -> 0% of each run, Pallas kernels for 0% -> 0%
where the time goes in v1:
time: 49.6 us; the launch traced here: 49.4 us
  Pallas kernels  45.6 us (92%)
  local copies, waits for them, and re-layouts  3.09 us (6%)
  between operations  0.64 us (1%)
    pallas_call x1, Pallas kernels, on_device(): pl.pallas_call(functools.partial(kernel, z), out_shape=(jax.ShapeDtypeStr...  45.6 us
    unnamed x2, local copies, waits for them, and re-layouts  3.09 us

profile of v1, /device:TPU:0, one launch (start us, length us, event | category | flops | bytes accessed | tf_op | source)
XLA Modules:
  0.0 49.4 jit_solution(6556633070104587532)
XLA Ops:
  0.6 45.6 %shard_map.86 = (bf16[256,256]{1,0:T(8,128)(2,1)}, f32[80,256]{1,0:T(8,128)}) custom-call(bf16[256,2560]{1,0:T(8,128)(2,1)} %bitcast.8, bf16[256,2560]{1,0:T(8,128)(2,1)} %bitcast.9, bf16[256,2560]{1,0:T(8,128)(2,1)} %bitcast.10, bf16[2560,128]{1,0:T(8,128)(2,1)} %bitcast.11, f32[40,256]{1,0:T(8,128)} %bitcast.14, f32[40,256]{1,0:T(8,128)} %bitcast.15, ...), custom_call_target="tpu_custom_call" | custom-call | tf_op jit(solution)/shard_map/pallas_call | solution.py:430
  46.3 1.6 %copy.11 = bf16[1,256,256]{2,1,0:T(8,128)(2,1)} copy(bf16[1,256,256]{2,1,0:T(8,128)(2,1)} %bitcast.13) | data formatting | bytes 262144
  47.8 1.5 %copy.12 = f32[80,256]{1,0:T(8,128)} copy(f32[80,256]{1,0:T(8,128)} %get-tuple-element.9) | data formatting | bytes 163840

commit v2 on v1

--- a/solution.py
+++ b/solution.py
@@ -16,9 +16,9 @@
 EPSILON = 1e-06
 
 
-def nt(a, b, precision=None):
+def nt(a, b):
     return lax.dot_general(
-        a, b, (((1,), (1,)), ((), ())), preferred_element_type=F32, precision=precision
+        a, b, (((1,), (1,)), ((), ())), preferred_element_type=F32
     )
 
 
@@ -47,6 +47,7 @@
         self.wide_pad = -(-self.wide // 16) * 16
         self.rows_seq = width // n_seq
         self.rows = self.rows_seq // n_dp
+        self.streams = 2 if n_dp % 2 == 0 else 1
 
 
 def kernel(
@@ -55,9 +56,9 @@
     grad_out, weight_out,
     layer, scan, cot, entry, local_sem,
     crow, ccol, wcol, wcot, win,
-    fsend, frecv, fown, fhigh, fsum, bsum, dsend, drecv, beyond, bsend, brecv,
+    fsend, frecv, fown, fhigh, fsum, bsum, dsend, drecv, bsend, brecv,
     fsem_s, fsem_r, dsem_s, dsem_r, bsem_s, bsem_r,
-    mix, part, wsend, wrecv, wsem_s, wsem_r, zsend, zrecv, zown, zsem_s, zsem_r,
+    mix, layer_t, part, wsend, wrecv, wsem_s, wsem_r, zsend, zrecv, zown, zsem_s, zsem_r,
     peak, peak_send, peak_recv, peak_send2, peak_recv2, pkcol,
     psem_s, psem_r, qsem_s, qsem_r,
 ):
@@ -89,10 +90,12 @@
     decay = decay_ref[...] * LOG2E
     row = lax.broadcasted_iota(jnp.int32, (t, t), 0)
     col = lax.broadcasted_iota(jnp.int32, (t, t), 1)
-    lower = jnp.where(col <= row, 1.0, 0.0).astype(F32)
-    high = lax.Precision.HIGHEST
-    cum = nt(decay, lower, high)
-    cum_t = nt(lower, decay, high)
+    lower = jnp.where(col <= row, 1.0, 0.0).astype(BF16)
+    cum = cum_t = 0.0
+    for _ in range(3):
+        piece = decay.astype(BF16)
+        decay = decay - piece.astype(F32)
+        cum, cum_t = cum + nt(piece, lower), cum_t + nt(lower, piece)
     steps = step_ref[...]
     crow[...] = cum - jnp.log2(steps)
     weight_t = jnp.transpose(steps) * jnp.exp2(cum_t[t - 1 : t, :] - cum_t)
@@ -224,14 +227,159 @@
                     mix[s * hf : (s + 1) * hf, cut] += scores[:, cut] * jnp.exp2(spread_)
         return carry
 
-    lax.fori_loop(0, z.heads // z.per, mixing, 0)
+    fills = [
+        (i * (z.heads // z.per) // z.chunks, (i + 1) * (z.heads // z.per) // z.chunks)
+        for i in range(z.chunks)
+    ]
+
+    def fill():
+        if fills:
+            lax.fori_loop(*fills.pop(0), mixing, 0)
+
+    slope = sigma * (1.0 + pre * (1.0 - sigma))
+    states, half = z.states, z.rows_seq // z.streams
+    order = {}
+    for q in range(2):
+        for i in range(z.streams):
+            rest = list(range(1, z.bits))
+            order[q, i] = [0] + (rest[::-1] if q == 0 and i == 1 else rest)
+    number = {key: i for i, key in enumerate(order)}
+    offset = [sum(n >> (k + 1) for k in range(i)) for i in range(z.bits)]
+
+    def spot(u, key):
+        r = 0
+        for b in order[key][1:]:
+            r = 2 * r + ((u >> (b - 1)) & 1)
+        return r
+
+    def w_copy(key, k):
+        at, w = pl.ds(offset[k], n >> (k + 1)), number[key]
+        return remote(
+            wsend.at[w, at], wrecv.at[w, at], wsem_s.at[w, k], wsem_r.at[w, k],
+            mate[order[key][k]], dz,
+        )
+
+    def w_begin(q, grads):
+        def block(u, low):
+            s = 2 * u + low
+            at = pl.ds(pl.multiple_of(s * z.rows_seq, 16), z.rows_seq)
+            return nn(layer_t[at, :], grads)
+
+        for u in range(n // 2):
+            value = block(u, other).astype(BF16)
+            for i in range(z.streams):
+                wsend[number[q, i], spot(u, (q, i))] = value[i * half : (i + 1) * half]
+        for i in range(z.streams):
+            go(w_copy((q, i), 0))
+        for u in range(n // 2):
+            value = block(u, mine)
+            for i in range(z.streams):
+                part[number[q, i], spot(u, (q, i))] = value[i * half : (i + 1) * half]
+
+    starts = {key: 0 for key in order}
+
+    def w_step(key, k):
+        w_copy(key, k).wait_recv()
+        w, start = number[key], starts[key]
+        size = n >> (k + 1)
+        if k + 1 < z.bits:
+            away_size = size // 2
+            b = bit[order[key][k + 1]]
+            away, kept = (1 - b) * away_size, b * away_size
+            for j in range(away_size):
+                value = part[w, start + away + j] + wrecv[w, offset[k] + away + j].astype(F32)
+                wsend[w, offset[k + 1] + j] = value.astype(BF16)
+            go(w_copy(key, k + 1))
+            for j in range(away_size):
+                part[w, start + kept + j] += wrecv[w, offset[k] + kept + j].astype(F32)
+            starts[key] = start + kept
+            return
+        value = part[w, start] + wrecv[w, offset[k]].astype(F32)
+        first = me * z.rows_seq + key[1] * half
+        scale = 1.0 / (pkcol[pl.ds(pl.multiple_of(first, 8), half), :] + EPSILON)
+        value = value * scale
+        base, count = key[1] * m // z.streams, m // z.streams
+        for d in range(count):
+            piece = value[d * z.rows : (d + 1) * z.rows, :]
+            zsend[key[0], base + d] = piece.astype(BF16)
+            zown[key[0], base + d] = piece
+
+    def z_copy(q, o):
+        to = lax.rem(dz + o, m)
+        return remote(
+            zsend.at[q, to], zrecv.at[q, o - 1], zsem_s.at[q, o - 1], zsem_r.at[q, o - 1], me, to
+        )
+
+    def w_cross(q):
+        for o in range(m - 1, 0, -1):
+            go(z_copy(q, o))
+
+    def w_end(q):
+        value = zown[q, dz]
+        for o in range(1, m):
+            z_copy(q, o).wait_recv()
+            value += zrecv[q, o - 1].astype(F32)
+        weight_out[:, q * states : (q + 1) * states] = value
+
+    acc = []
+    b_copies = []
+
+    def early():
+        while fills:
+            fill()
+        top = peak[...]
+        for o in range(1, n):
+            peak_copies[o - 1].wait_recv()
+            top = jnp.maximum(top, peak_recv[o - 1].astype(F32))
+        peak_send2[...] = top.astype(BF16)
+        peak_copies2 = [
+            go(remote(peak_send2, peak_recv2.at[o - 1], qsem_s.at[o - 1], qsem_r.at[o - 1],
+                      me, lax.rem(dz + o, m)))
+            for o in range(1, m)
+        ]
+        mixed = mix[...].astype(BF16)
+        acc.append(tn(mixed, reads))
+        locals_[3].wait()
+        grad_read = nn(mixed, writes) + nn(wcot[...], entry[...])
+        reads_grad = (grad_read * slope[:, states:]).astype(BF16)
+        grad_out[:, states:] = reads_grad
+        layer_t[...] = jnp.transpose(layer[...])
+        w_begin(1, reads_grad)
+        for i in range(z.streams):
+            w_step((1, i), 0)
+        for o in range(1, m):
+            peak_copies2[o - 1].wait_recv()
+            top = jnp.maximum(top, peak_recv2[o - 1].astype(F32))
+        unit = jnp.where(
+            lax.broadcasted_iota(jnp.int32, (LANES, LANES), 0)
+            == lax.broadcasted_iota(jnp.int32, (LANES, LANES), 1), 1.0, 0.0,
+        ).astype(BF16)
+        turned = nt(unit, top.astype(BF16))
+        for j in range(z.wide):
+            pkcol[j * LANES : (j + 1) * LANES, :] = jnp.broadcast_to(
+                turned[:, j : j + 1], (LANES, LANES)
+            )
+
+    def carried(side, c, state):
+        at = pl.multiple_of(side * (z.channels // 2) + c * z.chunk_rows, LANES)
+        return nn(win[:, pl.ds(at, z.chunk_rows)], state)
+
+    def finish(c, above):
+        low = fhigh[c] + spread(tot_high, c) * above
+        bsend[c] = jnp.where(mine == 1, low, above).astype(BF16)
+        b_copies.append(
+            go(remote(bsend.at[c], brecv.at[c], bsem_s.at[c], bsem_r.at[c], mate[0], dz))
+        )
+        acc[0] += carried(mine, c, jnp.where(mine == 1, above, low).astype(BF16))
 
     e_now = None
     for b in range(1, z.bits):
+        last = b == z.bits - 1
+        if last:
+            early()
         d_copy(b).wait_recv()
         d_far = drecv[b]
         d_low = jnp.where(bit[b] == 1, d_far, d_now)
-        last = b == z.bits - 1
         if not last:
             dsend[b + 1] = d_now * d_far
             go(d_copy(b + 1))
@@ -240,151 +388,57 @@
             far = frecv[b, c].astype(F32)
             scaled = far if e_now is None else spread(e_now, c) * far
             gained = bsum[c] + jnp.where(bit[b] == 1, jnp.zeros_like(scaled), scaled)
-            if not last:
-                bsum[c] = gained
-                own = fsum[c]
-                value = jnp.where(bit[b] == 1, far, own) + spread(d_low, c) * jnp.where(
-                    bit[b] == 1, own, far
-                )
-                fsum[c] = value
-                fsend[b + 1, c] = value.astype(BF16)
-                go(f_copy(b + 1, c))
-            else:
-                bsum[c] = gained
+            if last:
+                finish(c, gained)
+                continue
+            bsum[c] = gained
+            own = fsum[c]
+            value = jnp.where(bit[b] == 1, far, own) + spread(d_low, c) * jnp.where(
+                bit[b] == 1, own, far
+            )
+            fsum[c] = value
+            fsend[b + 1, c] = value.astype(BF16)
+            go(f_copy(b + 1, c))
+            if b == 1:
+                fill()
         one = jnp.ones_like(d_far) if e_now is None else e_now
         e_now = jnp.where(bit[b] == 1, one, one * d_far)
         d_now = d_now * d_far
-    for o in range(1, n):
-        peak_copies[o - 1].wait_recv()
-
-    b_copies = []
-    mixed = mix[...].astype(BF16)
-    grad_write = tn(mixed, reads)
-    for c in range(z.chunks):
-        top = bsum[c]
-        low = fhigh[c] + spread(tot_high, c) * top
-        beyond[c] = jnp.where(mine == 1, top, low).astype(BF16)
-        bsend[c] = jnp.where(mine == 1, low, top).astype(BF16)
-        b_copies.append(
-            go(remote(bsend.at[c], brecv.at[c], bsem_s.at[c], bsem_r.at[c], mate[0], dz))
-        )
-
-    slope = sigma * (1.0 + pre * (1.0 - sigma))
-    order = {1: list(range(z.bits)), 0: [0] + list(range(1, z.bits))[::-1]}
-    states = z.states
-
-    def place(r, q):
-        s = 0
-        for k, b in enumerate(order[q]):
-            s += ((r >> (z.bits - 1 - k)) & 1) << b
-        return s
-
-    offset = [sum(n >> (k + 1) for k in range(i)) for i in range(z.bits)]
-
-    def w_copy(q, k):
-        size = n >> (k + 1)
-        at = pl.ds(offset[k], size)
-        return remote(
-            wsend.at[q, at], wrecv.at[q, at], wsem_s.at[q, k], wsem_r.at[q, k],
-            mate[order[q][k]], dz,
-        )
-
-    def w_send(q, k, start):
-        size = n >> (k + 1)
-        b = bit[order[q][k]]
-        away, kept = start + (1 - b) * size, start + b * size
-        for j in range(size):
-            wsend[q, offset[k] + j] = part[q, away + j].astype(BF16)
-        go(w_copy(q, k))
-        return kept
-
-    def w_begin(q, grads):
-        product = tn(layer[...], grads)
-        for r in range(n):
-            s = place(r, q)
-            part[q, r] = product[s * z.rows_seq : (s + 1) * z.rows_seq, :]
-        return w_send(q, 0, 0)
-
-    def w_step(q, k, start):
-        w_copy(q, k).wait_recv()
-        size = n >> (k + 1)
-        for j in range(size):
-            part[q, start + j] += wrecv[q, offset[k] + j].astype(F32)
-        if k + 1 < z.bits:
-            return w_send(q, k + 1, start)
-        scale = 1.0 / (pkcol[pl.ds(pl.multiple_of(me * z.rows_seq, 8), z.rows_seq), :] + EPSILON)
-        value = part[q, start] * scale
-        for d in range(m):
-            piece = value[d * z.rows : (d + 1) * z.rows, :]
-            zsend[q, d] = piece.astype(BF16)
-            zown[q, d] = piece
-        for o in range(1, m):
-            go(z_copy(q, o))
-        return start
-
-    def z_copy(q, o):
-        to = lax.rem(dz + o, m)
-        return remote(
-            zsend.at[q, to], zrecv.at[q, o - 1], zsem_s.at[q, o - 1], zsem_r.at[q, o - 1], me, to
-        )
-
-    def w_end(q):
-        value = zown[q, dz]
-        for o in range(1, m):
-            z_copy(q, o).wait_recv()
-            value += zrecv[q, o - 1].astype(F32)
-        weight_out[:, q * states : (q + 1) * states] = value
-
-    locals_[3].wait()
-    grad_read = nn(mixed, writes) + nn(wcot[...], entry[...])
-    reads_grad = (grad_read * slope[:, states:]).astype(BF16)
-    grad_out[:, states:] = reads_grad
-    at_read = w_begin(1, reads_grad)
-
-    top = peak[...]
-    for o in range(1, n):
-        top = jnp.maximum(top, peak_recv[o - 1].astype(F32))
-    peak_send2[...] = top.astype(BF16)
-    peak_copies2 = [
-        go(remote(peak_send2, peak_recv2.at[o - 1], qsem_s.at[o - 1], qsem_r.at[o - 1],
-                  me, lax.rem(dz + o, m)))
-        for o in range(1, m)
-    ]
-
-    def carried(half, c, state):
-        width = z.chunk_rows
-        at = pl.multiple_of(half * (z.channels // 2) + c * width, LANES)
-        return nn(win[:, pl.ds(at, width)], state)
-
-    for c in range(z.chunks):
-        grad_write += carried(mine, c, beyond[c])
+    if z.bits == 1:
+        early()
+        for c in range(z.chunks):
+            finish(c, bsum[c])
+
+    keys = {q: [(q, i) for i in range(z.streams)] for q in range(2)}
+    if z.bits > 1:
+        for key in keys[1]:
+            w_step(key, 1)
+    grad_write = acc[0]
     for c in range(z.chunks):
         b_copies[c].wait_recv()
         grad_write += carried(other, c, brecv[c])
     writes_grad = (grad_write * slope[:, :states]).astype(BF16)
+    w_begin(0, writes_grad)
     grad_out[:, :states] = writes_grad
-    at_write = w_begin(0, writes_grad)
-
-    for o in range(1, m):
-        peak_copies2[o - 1].wait_recv()
-        top = jnp.maximum(top, peak_recv2[o - 1].astype(F32))
-    unit = jnp.where(
-        lax.broadcasted_iota(jnp.int32, (LANES, LANES), 0)
-        == lax.broadcasted_iota(jnp.int32, (LANES, LANES), 1), 1.0, 0.0,
-    ).astype(BF16)
-    turned = nt(unit, top.astype(BF16))
-    for j in range(z.wide):
-        pkcol[j * LANES : (j + 1) * LANES, :] = jnp.broadcast_to(
-            turned[:, j : j + 1], (LANES, LANES)
-        )
-
     for k in range(z.bits):
-        at_read = w_step(1, k, at_read)
-        at_write = w_step(0, k, at_write)
+        for key in keys[0]:
+            w_step(key, k)
+        if k + 1 == z.bits:
+            w_cross(0)
+        if k + 2 < z.bits:
+            for key in keys[1]:
+                w_step(key, k + 2)
+        if k + 3 == z.bits or (k == 0 and z.bits < 3):
+            w_cross(1)
     w_end(1)
     w_end(0)
     for copy in started:
         copy.wait_send()
+
+
+def settle(grads, weights, grads_out, weights_out):
+    grads_out[0] = grads[...]
+    weights_out[...] = weights[...]
 
 
 def solution(mesh):
@@ -399,10 +453,10 @@
         z = Sizes(n_seq, n_dp, tokens, width, channels, heads, states)
         dma = pltpu.SemaphoreType.DMA
         chunk = (z.chunks, z.chunk_rows, states)
-        steps_w = n_seq - 1
+        steps_w, flows = n_seq - 1, 2 * z.streams
         peers, mates = max(n_dp - 1, 1), max(n_seq - 1, 1)
         peak = (z.wide_pad, LANES)
-        block = (z.rows_seq, states)
+        block = (z.rows_seq // z.streams, states)
         piece = (z.rows, states)
         V = pltpu.VMEM
         scratch = [
@@ -413,12 +467,13 @@
             V((tokens, channels), BF16),
             V((z.bits,) + chunk, BF16), V((z.bits,) + chunk, BF16), V(chunk, F32), V(chunk, F32),
             V(chunk, F32), V(chunk, F32), V((z.bits, z.half_heads, LANES), F32),
-            V((z.bits, z.half_heads, LANES), F32), V(chunk, BF16), V(chunk, BF16), V(chunk, BF16),
+            V((z.bits, z.half_heads, LANES), F32), V(chunk, BF16), V(chunk, BF16),
             dma((z.bits, z.chunks)), dma((z.bits, z.chunks)), dma((z.bits,)), dma((z.bits,)),
             dma((z.chunks,)), dma((z.chunks,)),
-            V((tokens, tokens), F32), V((2, n_seq) + block, F32),
-            V((2, steps_w) + block, BF16), V((2, steps_w) + block, BF16),
-            dma((2, z.bits)), dma((2, z.bits)),
+            V((tokens, tokens), F32), V((width, tokens), BF16),
+            V((flows, n_seq // 2) + block, F32),
+            V((flows, steps_w) + block, BF16), V((flows, steps_w) + block, BF16),
+            dma((flows, z.bits)), dma((flows, z.bits)),
             V((2, n_dp) + piece, BF16), V((2, peers) + piece, BF16), V((2, n_dp) + piece, F32),
             dma((2, peers)), dma((2, peers)),
             V(peak, F32), V(peak, BF16), V((mates,) + peak, BF16), V(peak, BF16),
@@ -443,7 +498,15 @@
             layer_input[0], scan_input[0], scan_cotangent[0], entry_state[0, 0],
             step_size[0], log_decay[0], state_inputs[0],
         )
-        return grads[None], weights
+        return pl.pallas_call(
+            settle,
+            out_shape=(
+                jax.ShapeDtypeStruct((1,) + grads.shape, BF16),
+                jax.ShapeDtypeStruct(weights.shape, F32),
+            ),
+            in_specs=[vmem, vmem],
+            out_specs=(vmem, vmem),
+        )(grads, weights)
 
     placed = (
         P("dp", "seq", None),

time: 49.6 us -> 44 us (0.89)
  local copies, waits for them, and re-layouts: 3.09 us -> 0 us
  Pallas kernels: 45.6 us -> 43.2 us
    pallas_call x1, Pallas kernels: 45.6 us -> 41.5 us  [on_device(): pl.pallas_call(functools.partial(kernel, z), out_shape=(jax.ShapeDtypeStr...]
    unnamed x2 -> x0, local copies, waits for them, and re-layouts: 3.09 us -> none
    pallas_call x0 -> x1, Pallas kernels: none -> 1.64 us  [on_device(): pl.pallas_call(settle, out_shape=(jax.ShapeDtypeStruct((1,) + grads.shape...]
where the time goes in v2:
time: 44 us; the launch traced here: 43.8 us
  Pallas kernels  43.2 us (98%)
  between operations  0.64 us (1%)
    pallas_call x1, Pallas kernels, on_device(): pl.pallas_call(functools.partial(kernel, z), out_shape=(jax.ShapeDtypeStr...  41.5 us
    pallas_call x1, Pallas kernels, on_device(): pl.pallas_call(settle, out_shape=(jax.ShapeDtypeStruct((1,) + grads.shape...  1.64 us

profile of v2, /device:TPU:0, one launch (start us, length us, event | category | flops | bytes accessed | tf_op | source)
XLA Modules:
  0.0 43.8 jit_solution(9175810650544774501)
XLA Ops:
  0.6 41.5 %shard_map.86 = (bf16[256,256]{1,0:T(8,128)(2,1)}, f32[80,256]{1,0:T(8,128)}) custom-call(bf16[256,2560]{1,0:T(8,128)(2,1)} %bitcast.7, bf16[256,2560]{1,0:T(8,128)(2,1)} %bitcast.8, bf16[256,2560]{1,0:T(8,128)(2,1)} %bitcast.9, bf16[2560,128]{1,0:T(8,128)(2,1)} %bitcast.10, f32[40,256]{1,0:T(8,128)} %bitcast.12, f32[40,256]{1,0:T(8,128)} %bitcast.13, ...), custom_call_target="tpu_custom_call" | custom-call | tf_op jit(solution)/shard_map/pallas_call | solution.py:485
  42.2 1.6 %shard_map.87 = (bf16[1,256,256]{2,1,0:T(8,128)(2,1)}, f32[80,256]{1,0:T(8,128)}) custom-call(bf16[256,256]{1,0:T(8,128)(2,1)} %get-tuple-element.4.grads, f32[80,256]{1,0:T(8,128)} %get-tuple-element.5.weights), custom_call_target="tpu_custom_call" | custom-call | tf_op jit(solution)/shard_map/pallas_call | solution.py:501

commit v3 on v2

--- a/solution.py
+++ b/solution.py
@@ -321,7 +321,7 @@
             value += zrecv[q, o - 1].astype(F32)
         weight_out[:, q * states : (q + 1) * states] = value
 
-    acc = []
+    acc, tops = [], []
     b_copies = []
 
     def early():
@@ -331,12 +331,13 @@
         for o in range(1, n):
             peak_copies[o - 1].wait_recv()
             top = jnp.maximum(top, peak_recv[o - 1].astype(F32))
+        tops.append(top)
         peak_send2[...] = top.astype(BF16)
-        peak_copies2 = [
-            go(remote(peak_send2, peak_recv2.at[o - 1], qsem_s.at[o - 1], qsem_r.at[o - 1],
-                      me, lax.rem(dz + o, m)))
-            for o in range(1, m)
-        ]
+        for o in range(1, m):
+            tops.append(
+                go(remote(peak_send2, peak_recv2.at[o - 1], qsem_s.at[o - 1], qsem_r.at[o - 1],
+                          me, lax.rem(dz + o, m)))
+            )
         mixed = mix[...].astype(BF16)
         acc.append(tn(mixed, reads))
         locals_[3].wait()
@@ -345,10 +346,15 @@
         grad_out[:, states:] = reads_grad
         layer_t[...] = jnp.transpose(layer[...])
         w_begin(1, reads_grad)
+
+    def forward():
         for i in range(z.streams):
             w_step((1, i), 0)
+
+    def columns():
+        top = tops[0]
         for o in range(1, m):
-            peak_copies2[o - 1].wait_recv()
+            tops[o].wait_recv()
             top = jnp.maximum(top, peak_recv2[o - 1].astype(F32))
         unit = jnp.where(
             lax.broadcasted_iota(jnp.int32, (LANES, LANES), 0)
@@ -390,6 +396,8 @@
             gained = bsum[c] + jnp.where(bit[b] == 1, jnp.zeros_like(scaled), scaled)
             if last:
                 finish(c, gained)
+                if c == z.chunks // 2:
+                    forward()
                 continue
             bsum[c] = gained
             own = fsum[c]
@@ -408,11 +416,9 @@
         early()
         for c in range(z.chunks):
             finish(c, bsum[c])
+        forward()
 
     keys = {q: [(q, i) for i in range(z.streams)] for q in range(2)}
-    if z.bits > 1:
-        for key in keys[1]:
-            w_step(key, 1)
     grad_write = acc[0]
     for c in range(z.chunks):
         b_copies[c].wait_recv()
@@ -421,14 +427,18 @@
     w_begin(0, writes_grad)
     grad_out[:, :states] = writes_grad
     for k in range(z.bits):
+        if k + 1 == z.bits and k == 0:
+            columns()
         for key in keys[0]:
             w_step(key, k)
+        if k == 0 and z.bits > 1:
+            columns()
         if k + 1 == z.bits:
             w_cross(0)
-        if k + 2 < z.bits:
+        if k + 1 < z.bits:
             for key in keys[1]:
-                w_step(key, k + 2)
-        if k + 3 == z.bits or (k == 0 and z.bits < 3):
+                w_step(key, k + 1)
+        if k + 2 == z.bits or z.bits == 1:
             w_cross(1)
     w_end(1)
     w_end(0)

time: 44 us -> 39.9 us (0.907)
  Pallas kernels: 43.2 us -> 39.1 us
    pallas_call x1, Pallas kernels: 41.5 us -> 37.5 us  [on_device(): pl.pallas_call(functools.partial(kernel, z), out_shape=(jax.ShapeDtypeStr...]
where the time goes in v3:
time: 39.9 us; the launch traced here: 39.8 us
  Pallas kernels  39.1 us (98%)
  between operations  0.64 us (2%)
    pallas_call x1, Pallas kernels, on_device(): pl.pallas_call(functools.partial(kernel, z), out_shape=(jax.ShapeDtypeStr...  37.5 us
    pallas_call x1, Pallas kernels, on_device(): pl.pallas_call(settle, out_shape=(jax.ShapeDtypeStruct((1,) + grads.shape...  1.64 us

profile of v3, /device:TPU:0, one launch (start us, length us, event | category | flops | bytes accessed | tf_op | source)
XLA Modules:
  0.0 39.8 jit_solution(4043521522557852177)
XLA Ops:
  0.6 37.5 %shard_map.86 = (bf16[256,256]{1,0:T(8,128)(2,1)}, f32[80,256]{1,0:T(8,128)}) custom-call(bf16[256,2560]{1,0:T(8,128)(2,1)} %bitcast.7, bf16[256,2560]{1,0:T(8,128)(2,1)} %bitcast.8, bf16[256,2560]{1,0:T(8,128)(2,1)} %bitcast.9, bf16[2560,128]{1,0:T(8,128)(2,1)} %bitcast.10, f32[40,256]{1,0:T(8,128)} %bitcast.12, f32[40,256]{1,0:T(8,128)} %bitcast.13, ...), custom_call_target="tpu_custom_call" | custom-call | tf_op jit(solution)/shard_map/pallas_call | solution.py:495
  38.1 1.6 %shard_map.87 = (bf16[1,256,256]{2,1,0:T(8,128)(2,1)}, f32[80,256]{1,0:T(8,128)}) custom-call(bf16[256,256]{1,0:T(8,128)(2,1)} %get-tuple-element.4.grads, f32[80,256]{1,0:T(8,128)} %get-tuple-element.5.weights), custom_call_target="tpu_custom_call" | custom-call | tf_op jit(solution)/shard_map/pallas_call | solution.py:511
